TPU v7x, 32 devices: a whole 2x2x4 slice. The times are simulated.
32 devices in a mesh: angle: 4 (over z), pos: 8 (over y, x, core).
Axes of the slice: x: 2, y: 2, z: 4, core: 2. Of those that a mesh axis runs over, the one named last changes fastest.
Arguments:
- amplitude: float32 [4, 32, 128, 128], P('angle', 'pos'), may hold values from 0 to 2.5
- offsets: int32 [4, 32, 2], P('angle', 'pos'), may hold values from 0 to 896, as said below
- probe_field: float32 [2, 128, 128], replicated, may hold values from -5 to 5
- object_field: float32 [4, 2, 1024, 1024], P('angle', None, 'pos'), may hold values from -5 to 5
- interp_index: int32 [4, 2, 1024], replicated, may hold values from 0 to 1022
- interp_weight: float32 [4, 2, 1024], replicated, may hold values from 0 to 1
Outputs:
- new_object: float32 [4, 2, 1024, 1024], P('angle', None, 'pos')
- new_probe: float32 [2, 128, 128], replicated
- recon: float32 [8, 128, 2, 1024], P('pos', 'angle')
Inputs may be any that keep to these rules, and one draw needn't show every extreme that they name: For position j, offsets[a, j, 0] = max(0, min(896, (j // 4) * 128 - 128 // 2 + u)) with 0 <= u < 128; offsets[a, j, 1] lies in 0 to 896.
All inputs are finite; a program needn't handle non-finite values.
Results may differ from a plain program's by a relative error of at most 0.00007.
Values sent between devices are 32-bit elements; how exact they have to be, the bound alone decides.
A program may use at most 64 MiB of HBM per device.

v0:
```python
import math

import jax
import jax.numpy as jnp
from jax import lax
from jax.sharding import PartitionSpec as P


def with_halo(block, sides, width):
    for axis, dim in sides:
        count = lax.axis_size(axis)
        forward = [(i, i + 1) for i in range(count - 1)]
        backward = [(target, source) for source, target in forward]
        low = lax.ppermute(
            lax.slice_in_dim(block, block.shape[dim] - width, None, axis=dim), axis, forward
        )
        high = lax.ppermute(lax.slice_in_dim(block, 0, width, axis=dim), axis, backward)
        block = jnp.concatenate([low, block, high], axis=dim)
    return block


def passed_along(array, axis, by):
    length = lax.axis_size(axis)
    pairs = [(i, i + by) for i in range(length) if 0 <= i + by < length]
    return lax.ppermute(array, axis, pairs)


def ramp_matrix(length):
    ramp = jnp.arange(length, dtype=jnp.int32)
    differ = ramp[:, None] - ramp[None, :]
    spread = differ.astype(jnp.float32)
    squared = jnp.maximum(spread * spread, 1.0)
    odd_terms = jnp.where(differ % 2 != 0, -1.0 / (math.pi * math.pi * squared), 0.0)
    return jnp.where(differ == 0, 0.25, odd_terms)


def dft_tables(length):
    ramp = jnp.arange(length, dtype=jnp.int32)
    phases = ramp[:, None] * ramp[None, :] % length
    theta = phases.astype(jnp.float32) * (2.0 * math.pi / length)
    factor = 1.0 / math.sqrt(length)
    return (jnp.cos(theta) * factor, -jnp.sin(theta) * factor)


def left_product(table_real, table_imag, value_real, value_imag):
    high = lax.Precision.HIGHEST
    first = jnp.einsum("ij,bjk->bik", table_real, value_real, precision=high)
    second = jnp.einsum("ij,bjk->bik", table_imag, value_imag, precision=high)
    third = jnp.einsum("ij,bjk->bik", table_real, value_imag, precision=high)
    fourth = jnp.einsum("ij,bjk->bik", table_imag, value_real, precision=high)
    return (first - second, third + fourth)


def right_product(value_real, value_imag, table_real, table_imag):
    high = lax.Precision.HIGHEST
    first = jnp.einsum("bij,jk->bik", value_real, table_real, precision=high)
    second = jnp.einsum("bij,jk->bik", value_imag, table_imag, precision=high)
    third = jnp.einsum("bij,jk->bik", value_imag, table_real, precision=high)
    fourth = jnp.einsum("bij,jk->bik", value_real, table_imag, precision=high)
    return (first - second, third + fourth)


def transform_both(value_real, value_imag, table_real, table_imag):
    middle_real, middle_imag = left_product(table_real, table_imag, value_real, value_imag)
    return right_product(middle_real, middle_imag, table_real, table_imag)


def on_device(amplitude, offsets, probe_field, object_field, interp_index, interp_weight):
    band = object_field.shape[2]
    width = object_field.shape[3]
    patch = probe_field.shape[1]
    half_patch = patch // 2
    per_device = offsets.shape[1]
    row_index = lax.axis_index("pos")
    extended = with_halo(object_field, (("pos", 2),), half_patch)
    anchor = row_index * band - half_patch
    local_rows = offsets[:, :, 0] - anchor
    columns = offsets[:, :, 1]
    table_real, table_imag = dft_tables(patch)
    probe_real = probe_field[0]
    probe_imag = probe_field[1]
    power = probe_real * probe_real + probe_imag * probe_imag
    channels = 3

    def one_angle(inputs):
        amps, rows, cols, layer = inputs

        def take_patch(first_row, first_col):
            return lax.dynamic_slice(layer, (jnp.int32(0), first_row, first_col), (2, patch, patch))

        cut = jax.vmap(take_patch)(rows, cols)
        patch_real = cut[:, 0]
        patch_imag = cut[:, 1]
        wave_real = probe_real * patch_real - probe_imag * patch_imag
        wave_imag = probe_real * patch_imag + probe_imag * patch_real
        spec_real, spec_imag = transform_both(wave_real, wave_imag, table_real, table_imag)
        magnitude = jnp.sqrt(spec_real * spec_real + spec_imag * spec_imag)
        factor = amps / jnp.maximum(magnitude, 0.5)
        back_real, back_imag = transform_both(
            factor * spec_real, factor * spec_imag, table_real, -table_imag
        )
        diff_real = back_real - wave_real
        diff_imag = back_imag - wave_imag
        grad_real = probe_real * diff_real + probe_imag * diff_imag
        grad_imag = probe_real * diff_imag - probe_imag * diff_real
        numer_real = jnp.sum(patch_real * diff_real + patch_imag * diff_imag, axis=0)
        numer_imag = jnp.sum(patch_real * diff_imag - patch_imag * diff_real, axis=0)
        denom = jnp.sum(patch_real * patch_real + patch_imag * patch_imag, axis=0)
        pieces = [grad_real, grad_imag]
        pieces.append(jnp.broadcast_to(power, grad_real.shape))
        stacked = jnp.stack(pieces, axis=1)

        def accumulate(count, total):
            start = (jnp.int32(0), rows[count], cols[count])
            current = lax.dynamic_slice(total, start, (channels, patch, patch))
            return lax.dynamic_update_slice(total, current + stacked[count], start)

        total = lax.fori_loop(
            0, per_device, accumulate, jnp.zeros((channels, band + patch, width), jnp.float32)
        )
        return (total, jnp.stack([numer_real, numer_imag]), denom)

    buffers, numers, denoms = lax.map(one_angle, (amplitude, local_rows, columns, extended))
    upper_rims = buffers[:, :, :half_patch]
    lower_rims = buffers[:, :, half_patch + band :]
    from_below = passed_along(upper_rims, "pos", -1)
    from_above = passed_along(lower_rims, "pos", 1)
    owned = buffers[:, :, half_patch : half_patch + band]
    owned = owned.at[:, :, :half_patch].add(from_above)
    owned = owned.at[:, :, band - half_patch :].add(from_below)
    weight_sum = owned[:, 2]
    new_object = object_field + owned[:, :2] / (weight_sum[:, None] + 1.0)
    numer_all, denom_all = lax.psum(
        (jnp.sum(numers, axis=0), jnp.sum(denoms, axis=0)), ("angle", "pos")
    )
    new_probe = probe_field + numer_all / (denom_all + 1.0)
    regrouped = lax.all_to_all(new_object[:, 1], "angle", split_axis=1, concat_axis=0, tiled=True)
    total_angles = regrouped.shape[0]
    slice_count = regrouped.shape[1]
    sinogram = jnp.transpose(regrouped, (1, 0, 2))
    filtered = jnp.dot(
        sinogram.reshape(slice_count * total_angles, width),
        ramp_matrix(width),
        precision=lax.Precision.HIGHEST,
    )
    filtered = jnp.moveaxis(filtered.reshape(slice_count, total_angles, width), 1, 0)
    zwin = interp_index.shape[1]
    bins = jnp.arange(width, dtype=jnp.int32)[:, None]

    def back_step(total, inputs):
        rows_angle, index_angle, weight_angle = inputs
        results = []
        for depth in range(zwin):
            lower_bin = index_angle[depth][None, :]
            upper_weight = weight_angle[depth][None, :]
            matrix = jnp.where(bins == lower_bin, 1.0 - upper_weight, 0.0) + jnp.where(
                bins == lower_bin + 1, upper_weight, 0.0
            )
            results.append(jnp.dot(rows_angle, matrix, precision=lax.Precision.HIGHEST))
        return (total + jnp.concatenate(results, axis=1), None)

    total, unused = lax.scan(
        back_step,
        jnp.zeros((slice_count, zwin * width), jnp.float32),
        (filtered, interp_index, interp_weight),
    )
    recon = (total * (math.pi / total_angles)).reshape(1, slice_count, zwin, width)
    return (new_object, new_probe, recon)


def solution(mesh):
    placed = (
        P("angle", "pos", None, None),
        P("angle", "pos", None),
        P(),
        P("angle", None, "pos", None),
        P(),
        P(),
    )
    return jax.shard_map(
        on_device,
        mesh=mesh,
        in_specs=placed,
        out_specs=(P("angle", None, "pos", None), P(), P("pos", "angle", None, None)),
        check_vma=False,
    )
```

profile of v0, /device:TPU:0, one launch (start us, length us, event | category | flops | bytes accessed | tf_op | source)
XLA Modules:
  0.0 307.8 jit_solution(7285216097695240660)
XLA Ops:
  7.2 1.4 fusion.203
  8.5 2.4 collective-permute-start
  11.0 1.3 collective-permute-start.1
  12.3 0.8 compare_select_fusion.1
  13.1 0.8 slice_bitcast_fusion.3
  13.9 0.9 multiply_add_fusion
  14.8 0.9 slice_bitcast_fusion.2
  15.7 0.8 copy-done.5
  17.0 1.4 maximum_bitcast_fusion
  18.4 10.2 %while.38 = (s32[]{:T(128)}, f32[2,256,1024]{2,1,0:T(8,128)S(1)}, s32[4,3]{1,0:T(4,128)S(1)}, f32[4,2,128,128]{3,2,0,1:T(8,128)}, s32[]{:T(128)}) while((s32[]{:T(128)}, f32[2,256,1024]{2,1,0:T(8,128)S(1)}, s32[4,3]{1,0:T(4,128)S(1)}, f32[4,2,128,128]{3,2,0,1:T(8,128)}, s32[]{:T(128)}) %tuple.101), condition=%wide.while_cond.2, body=%wide.while_body.2.sunk | while | flops 2 | bytes 263785 | solution.py:89
  19.0 2.0 bitcast_dynamic-update-slice_fusion.2
  21.6 2.0 bitcast_dynamic-update-slice_fusion.2
  24.1 1.9 bitcast_dynamic-update-slice_fusion.2
  26.6 2.0 bitcast_dynamic-update-slice_fusion.2
  28.6 1.1 fusion.65
  35.6 0.8 fusion.91
  36.4 0.8 fusion.87
  37.3 0.8 fusion.59
  38.1 0.8 fusion.58
  40.5 0.7 fusion.56
  41.2 1.6 fusion.67
  42.9 0.9 pad_maximum_fusion
  44.2 35.4 %while.37 = (s32[]{:T(128)}, f32[3,256,1024]{2,1,0:T(8,128)S(1)}, s32[4]{0:T(128)S(1)}, s32[4]{0:T(128)S(1)}, f32[4,3,128,128]{3,2,0,1:T(8,128)}, /*index=5*/s32[]{:T(128)}, s32[]{:T(128)}, s32[]{:T(128)}, s32[]{:T(128)}) while((s32[]{:T(128)}, f32[3,256,1024]{2,1,0:T(8,128)S(1)}, s32[4]{0:T(128)S(1)}, s32[4]{0:T(128)S(1)}, ...), condition=%wide.region_1.2_spmd, body=%wide.region_0.1_spmd.sunk | while | flops 49160 | bytes 983241 | solution.py:118
  49.2 1.1 bitcast_add_fusion.2
  50.2 2.8 dynamic_update_slice.17
  58.1 1.1 bitcast_add_fusion.2
  59.1 2.7 dynamic_update_slice.17
  66.8 1.1 bitcast_add_fusion.2
  67.9 2.8 dynamic_update_slice.17
  75.7 1.1 bitcast_add_fusion.2
  76.8 2.8 dynamic_update_slice.17
  79.6 3.8 %broadcast_in_dim.70 = f32[1,3,256,1024]{3,0,2,1:T(1,128)} reshape(f32[3,256,1024]{2,1,0:T(8,128)S(1)} %get-tuple-element.208) | data formatting | bytes 6291456 | tf_op jit(solution)/shard_map/while/body/jit(dynamic_update_index_in_dim)/broadcast_in_dim | solution.py:123
  83.4 2.6 fusion.202
  86.0 12.3 %collective-permute-start.2 = (f32[1,3,64,1024]{3,0,2,1:T(1,128)S(1)}, f32[1,3,64,1024]{3,0,2,1:T(1,128)S(1)}, u32[]{:S(2)}, u32[]{:S(2)}) collective-permute-start(f32[1,3,64,1024]{3,0,2,1:T(1,128)S(1)} %get-tuple-element.326), channel_id=1, source_target_pairs={{0,1},{1,2},{2,3},{3,4},{4,5},{5,6},{6,7},{8,9},{9,10},{10,11},{11... | collective-permute-start | bytes 2359304 | tf_op jit(solution)/shard_map/ppermute | solution.py:25
  98.3 1.3 collective-permute-start.3
  100.2 0.9 fusion.63
  101.1 1.5 collective-permute-done.3
  102.5 0.9 fusion.62
  104.0 1.8 divide_add_fusion
  105.8 0.8 slice_bitcast_fusion
  106.6 4.9 %all-to-all-start = ((f32[1,128,1024]{2,0,1:T(1,128)}), f32[1,128,1024]{2,0,1:T(1,128)S(1)}, u32[]{:S(2)}, u32[]{:S(2)}) async-start(f32[1,128,1024]{2,0,1:T(1,128)} %slice_bitcast_fusion), calls=%async_computation | async-start | bytes 1048576 | tf_op jit(solution)/shard_map/all_to_all | solution.py:137
  112.2 144.5 %all-reduce.3.cloned.1.call-done = (f32[2,128,128]{2,1,0:T(8,128)}, f32[128,128]{1,0:T(8,128)}) async-done(((f32[2,128,128]{2,1,0:T(8,128)}, f32[128,128]{1,0:T(8,128)}), (f32[2,128,128]{2,1,0:T(8,128)}, f32[128,128]{1,0:T(8,128)})) %all-reduce.3.cloned.1.call-update) | async-done | bytes 196624 | tf_op jit(solution)/shard_map/psum | solution.py:133
  256.7 0.8 broadcast_add_fusion.2
  257.6 1.6 divide_add_fusion.1
  259.2 1.2 copy.70
  260.4 6.0 %fusion.53 = f32[4,32,1024]{2,1,0:T(8,128)S(1)} fusion(f32[32,4,1024]{2,0,1:T(8,128)S(1)} %bitcast.191), kind=kOutput, calls=%fused_computation.71 | convolution fusion | flops 1632632832 | bytes 1048576 | tf_op jit(solution)/shard_map/dot_general | solution.py:141
  266.5 33.6 %while.39 = (s32[]{:T(128)}, f32[32,2048]{1,0:T(8,128)S(1)}, f32[4,32,1024]{2,1,0:T(8,128)S(1)}, s32[4,2,1024]{2,1,0:T(2,128)}, f32[4,2,1024]{2,1,0:T(2,128)}, /*index=5*/s32[]{:T(128)}, s32[]{:T(128)}, s32[]{}) while((s32[]{:T(128)}, f32[32,2048]{1,0:T(8,128)S(1)}, f32[4,32,1024]{2,1,0:T(8,128)S(1)}, ...), condition=%wide.region_8.9_spmd.clone.clone, body=%wide.region_7.8_spmd.clone.clone.sunk | while | flops 815992832 | bytes 1409155 | solution.py:162
  266.5 0.8 constant_dynamic-slice_fusion.10
  267.3 0.8 constant_dynamic-slice_fusion.9
  268.1 3.3 %fusion.232 = f32[32,1024]{1,0:T(8,128)S(1)} fusion(f32[1024]{0:T(1024)S(1)} %bitcast.199, s32[1024]{0:T(1024)S(1)} %broadcast_add_fusion.6, f32[1024]{0:T(1024)S(1)} %broadcast_subtract_fusion.5, s32[1024]{0:T(1024)S(1)} %bitcast.197, f32[4,32,1024]{2,1,0:T(8,128)S(1)} %get-tuple-element.500, s32[]{:T(128)} %get-tuple-element.490), kind=kOutput, calls=%fused_computation.12.clone.1 | convolution fusion | flops 407896064 | bytes 278532 | tf_op jit(solution)/shard_map/while/body/eval_jaxpr/dot_general | solution.py:159
  271.4 3.3 %fusion.231 = f32[32,1024]{1,0:T(8,128)S(1)} fusion(f32[1024]{0:T(1024)S(1)} %bitcast.195, s32[1024]{0:T(1024)S(1)} %broadcast_add_fusion.5, f32[1024]{0:T(1024)S(1)} %broadcast_subtract_fusion.4, s32[1024]{0:T(1024)S(1)} %bitcast.193, f32[4,32,1024]{2,1,0:T(8,128)S(1)} %get-tuple-element.500, s32[]{:T(128)} %get-tuple-element.490), kind=kOutput, calls=%fused_computation.8.clone.1 | convolution fusion | flops 407896064 | bytes 278532 | tf_op jit(solution)/shard_map/while/body/eval_jaxpr/dot_general | solution.py:159
  274.9 0.8 constant_dynamic-slice_fusion.10
  275.7 0.8 constant_dynamic-slice_fusion.9
  276.5 3.3 %fusion.232 = f32[32,1024]{1,0:T(8,128)S(1)} fusion(f32[1024]{0:T(1024)S(1)} %bitcast.199, s32[1024]{0:T(1024)S(1)} %broadcast_add_fusion.6, f32[1024]{0:T(1024)S(1)} %broadcast_subtract_fusion.5, s32[1024]{0:T(1024)S(1)} %bitcast.197, f32[4,32,1024]{2,1,0:T(8,128)S(1)} %get-tuple-element.500, s32[]{:T(128)} %get-tuple-element.490), kind=kOutput, calls=%fused_computation.12.clone.1 | convolution fusion | flops 407896064 | bytes 278532 | tf_op jit(solution)/shard_map/while/body/eval_jaxpr/dot_general | solution.py:159
  279.8 3.3 %fusion.231 = f32[32,1024]{1,0:T(8,128)S(1)} fusion(f32[1024]{0:T(1024)S(1)} %bitcast.195, s32[1024]{0:T(1024)S(1)} %broadcast_add_fusion.5, f32[1024]{0:T(1024)S(1)} %broadcast_subtract_fusion.4, s32[1024]{0:T(1024)S(1)} %bitcast.193, f32[4,32,1024]{2,1,0:T(8,128)S(1)} %get-tuple-element.500, s32[]{:T(128)} %get-tuple-element.490), kind=kOutput, calls=%fused_computation.8.clone.1 | convolution fusion | flops 407896064 | bytes 278532 | tf_op jit(solution)/shard_map/while/body/eval_jaxpr/dot_general | solution.py:159
  283.3 0.8 constant_dynamic-slice_fusion.10
  284.1 0.8 constant_dynamic-slice_fusion.9
  284.9 3.3 %fusion.232 = f32[32,1024]{1,0:T(8,128)S(1)} fusion(f32[1024]{0:T(1024)S(1)} %bitcast.199, s32[1024]{0:T(1024)S(1)} %broadcast_add_fusion.6, f32[1024]{0:T(1024)S(1)} %broadcast_subtract_fusion.5, s32[1024]{0:T(1024)S(1)} %bitcast.197, f32[4,32,1024]{2,1,0:T(8,128)S(1)} %get-tuple-element.500, s32[]{:T(128)} %get-tuple-element.490), kind=kOutput, calls=%fused_computation.12.clone.1 | convolution fusion | flops 407896064 | bytes 278532 | tf_op jit(solution)/shard_map/while/body/eval_jaxpr/dot_general | solution.py:159
  288.2 3.3 %fusion.231 = f32[32,1024]{1,0:T(8,128)S(1)} fusion(f32[1024]{0:T(1024)S(1)} %bitcast.195, s32[1024]{0:T(1024)S(1)} %broadcast_add_fusion.5, f32[1024]{0:T(1024)S(1)} %broadcast_subtract_fusion.4, s32[1024]{0:T(1024)S(1)} %bitcast.193, f32[4,32,1024]{2,1,0:T(8,128)S(1)} %get-tuple-element.500, s32[]{:T(128)} %get-tuple-element.490), kind=kOutput, calls=%fused_computation.8.clone.1 | convolution fusion | flops 407896064 | bytes 278532 | tf_op jit(solution)/shard_map/while/body/eval_jaxpr/dot_general | solution.py:159
  291.7 0.8 constant_dynamic-slice_fusion.10
  292.5 0.8 constant_dynamic-slice_fusion.9
  293.2 3.3 %fusion.232 = f32[32,1024]{1,0:T(8,128)S(1)} fusion(f32[1024]{0:T(1024)S(1)} %bitcast.199, s32[1024]{0:T(1024)S(1)} %broadcast_add_fusion.6, f32[1024]{0:T(1024)S(1)} %broadcast_subtract_fusion.5, s32[1024]{0:T(1024)S(1)} %bitcast.197, f32[4,32,1024]{2,1,0:T(8,128)S(1)} %get-tuple-element.500, s32[]{:T(128)} %get-tuple-element.490), kind=kOutput, calls=%fused_computation.12.clone.1 | convolution fusion | flops 407896064 | bytes 278532 | tf_op jit(solution)/shard_map/while/body/eval_jaxpr/dot_general | solution.py:159
  296.6 3.3 %fusion.231 = f32[32,1024]{1,0:T(8,128)S(1)} fusion(f32[1024]{0:T(1024)S(1)} %bitcast.195, s32[1024]{0:T(1024)S(1)} %broadcast_add_fusion.5, f32[1024]{0:T(1024)S(1)} %broadcast_subtract_fusion.4, s32[1024]{0:T(1024)S(1)} %bitcast.193, f32[4,32,1024]{2,1,0:T(8,128)S(1)} %get-tuple-element.500, s32[]{:T(128)} %get-tuple-element.490), kind=kOutput, calls=%fused_computation.8.clone.1 | convolution fusion | flops 407896064 | bytes 278532 | tf_op jit(solution)/shard_map/while/body/eval_jaxpr/dot_general | solution.py:159
  300.1 0.9 reshape.185
  (79 shorter events, 17.7 us)
Async XLA Ops:
  7.2 9.8 %copy-start.1 = (f32[1,2,128,1024]{3,2,1,0:T(8,128)S(1)}, f32[1,2,128,1024]{3,2,1,0:T(8,128)}, u32[]{:S(2)}) copy-start(f32[1,2,128,1024]{3,2,1,0:T(8,128)} %param.17) | copy-start | bytes 3145732
  8.5 7.2 %collective-permute-start = (f32[1,2,64,1024]{3,2,1,0:T(8,128)S(1)}, f32[1,2,64,1024]{3,2,1,0:T(8,128)S(1)}, u32[]{:S(2)}, u32[]{:S(2)}) collective-permute-start(f32[1,2,64,1024]{3,2,1,0:T(8,128)S(1)} %get-tuple-element.327), channel_id=1, source_target_pairs={{0,1},{1,2},{2,3},{3,4},{4,5},{5,6},{6,7},{8,9},{9,10},{10,11},{11... | collective-permute-start | bytes 1572872 | tf_op jit(solution)/shard_map/ppermute | solution.py:14
  11.0 6.0 %collective-permute-start.1 = (f32[1,2,64,1024]{3,2,1,0:T(8,128)S(1)}, f32[1,2,64,1024]{3,2,1,0:T(8,128)}, u32[]{:S(2)}, u32[]{:S(2)}) collective-permute-start(f32[1,2,64,1024]{3,2,1,0:T(8,128)S(1)} %get-tuple-element.328), channel_id=1, source_target_pairs={{1,0},{2,1},{3,2},{4,3},{5,4},{6,5},{7,6},{9,8},{10,9},{11,10},{12... | collective-permute-start | bytes 1572872 | tf_op jit(solution)/shard_map/ppermute | solution.py:17
  15.7 0.8 copy-start.5
  28.6 7.0 %copy-start.6 = (f32[1,4,128,128]{3,2,1,0:T(8,128)S(1)}, f32[1,4,128,128]{3,2,1,0:T(8,128)}, u32[]{:S(2)}) copy-start(f32[1,4,128,128]{3,2,1,0:T(8,128)} %param.14) | copy-start | bytes 786436
  36.4 4.8 %copy-start.3 = (f32[4,2,128,128]{3,2,0,1:T(8,128)S(1)}, f32[4,2,128,128]{3,2,0,1:T(8,128)}, u32[]{:S(2)}) copy-start(f32[4,2,128,128]{3,2,0,1:T(8,128)} %get-tuple-element.217) | copy-start | bytes 1572868
  83.4 16.8 %copy-start = (f32[1,3,256,1024]{3,0,2,1:T(1,128)S(1)}, f32[1,3,256,1024]{3,0,2,1:T(1,128)}, u32[]{:S(2)}) copy-start(f32[1,3,256,1024]{3,0,2,1:T(1,128)} %broadcast_in_dim.70) | copy-start | bytes 9437188
  83.4 16.8 %slice-start = ((f32[1,3,256,1024]{3,0,2,1:T(1,128)}), f32[1,3,128,1024]{3,0,2,1:T(1,128)S(1)}, s32[]{:S(2)}) async-start(f32[1,3,256,1024]{3,0,2,1:T(1,128)} %broadcast_in_dim.70), calls=%async_computation.2 | async-start | bytes 3145728 | tf_op jit(solution)/shard_map/slice | solution.py:128
  86.0 14.2 %collective-permute-start.2 = (f32[1,3,64,1024]{3,0,2,1:T(1,128)S(1)}, f32[1,3,64,1024]{3,0,2,1:T(1,128)S(1)}, u32[]{:S(2)}, u32[]{:S(2)}) collective-permute-start(f32[1,3,64,1024]{3,0,2,1:T(1,128)S(1)} %get-tuple-element.326), channel_id=1, source_target_pairs={{0,1},{1,2},{2,3},{3,4},{4,5},{5,6},{6,7},{8,9},{9,10},{10,11},{11... | collective-permute-start | bytes 2359304 | tf_op jit(solution)/shard_map/ppermute | solution.py:25
  98.3 4.2 %collective-permute-start.3 = (f32[1,3,64,1024]{3,0,2,1:T(1,128)S(1)}, f32[1,3,64,1024]{3,0,2,1:T(1,128)S(1)}, u32[]{:S(2)}, u32[]{:S(2)}) collective-permute-start(f32[1,3,64,1024]{3,0,2,1:T(1,128)S(1)} %get-tuple-element.325), channel_id=1, source_target_pairs={{1,0},{2,1},{3,2},{4,3},{5,4},{6,5},{7,6},{9,8},{10,9},{11,10},{12... | collective-permute-start | bytes 2359304 | tf_op jit(solution)/shard_map/ppermute | solution.py:25
  99.6 4.3 %copy-start.2 = (f32[1,2,128,1024]{3,2,1,0:T(8,128)S(1)}, f32[1,2,128,1024]{3,2,1,0:T(8,128)}, u32[]{:S(2)}) copy-start(f32[1,2,128,1024]{3,2,1,0:T(8,128)} %param.17) | copy-start | bytes 3145732
  104.0 153.6 %copy-start.4 = (f32[2,128,128]{2,1,0:T(8,128)S(1)}, f32[2,128,128]{2,1,0:T(8,128)}, u32[]{:S(2)}) copy-start(f32[2,128,128]{2,1,0:T(8,128)} %param.16) | copy-start | bytes 393220
  106.6 153.7 %all-to-all-start = ((f32[1,128,1024]{2,0,1:T(1,128)}), f32[1,128,1024]{2,0,1:T(1,128)S(1)}, u32[]{:S(2)}, u32[]{:S(2)}) async-start(f32[1,128,1024]{2,0,1:T(1,128)} %slice_bitcast_fusion), calls=%async_computation | async-start | bytes 1048576 | tf_op jit(solution)/shard_map/all_to_all | solution.py:137
  111.5 145.2 %all-reduce.3.cloned.1.call-start = ((), (), s32[]{:S(2)}) async-start(), calls=%async_computation.1 | async-start | bytes 393216 | tf_op jit(solution)/shard_map/psum | solution.py:133
Sparse Core Ops, SparseCore 0:
  118.4 138.2 all-reduce.2
where the time goes:
time: 310 us; the launch traced here: 308 us
  waiting for transfers between devices  147 us (47%)
  local copies, waits for them, and re-layouts  45.6 us (15%)
  matrix products  45.6 us (15%)
  starting transfers between devices  22.2 us (7%)
  other arithmetic  17.6 us (6%)
  loops' own time  15.4 us (5%)
  between operations  14.4 us (5%)
    psum x1, waiting for transfers between devices, on_device(): lax.psum((jnp.sum(numers, axis=0), jnp.sum(denoms, axis=0)), ('angle', 'p...  145 us
    dot_general x8, matrix products, back_step(): results.append(jnp.dot(rows_angle, matrix, precision=lax.Precision.HIGHEST))  26.6 us
    another operation x1, loops' own time, one_angle(): lax.fori_loop(0, per_device, accumulate, jnp.zeros((channels, band + patc...  15.2 us
    ppermute x2, starting transfers between devices, passed_along(): return lax.ppermute(array, axis, pairs)  13.6 us
    dynamic_update_slice x4, local copies, waits for them, and re-layouts, accumulate(): return lax.dynamic_update_slice(total, current + stacked[count], start)  11.2 us
    gather x12, local copies, waits for them, and re-layouts  10.2 us
  transfers between devices with their start and end apart: 6, of which 4 were waited for; matrix products, arithmetic and copies ran while one was open for 3% of the time, Pallas kernels for 0%

commit v1 on v0

v1 whole, which is shorter than its diff:
```python
import functools
import math

import jax
import jax.numpy as jnp
import numpy as np
from jax import lax
from jax.experimental import pallas as pl
from jax.experimental.pallas import tpu as pltpu
from jax.sharding import PartitionSpec as P

MESH = pl.DeviceIdType.MESH
VMEM = pltpu.VMEM
BIG = 60 * 1024 * 1024


def split_const(table):
    high = jnp.asarray(table, jnp.float32).astype(jnp.bfloat16)
    low = (jnp.asarray(table, jnp.float32) - high.astype(jnp.float32)).astype(jnp.bfloat16)
    return high, low


def dft_blocks(length):
    ramp = np.arange(length)
    theta = (ramp[:, None] * ramp[None, :] % length) * (2.0 * math.pi / length)
    real = np.cos(theta) / math.sqrt(length)
    imag = -np.sin(theta) / math.sqrt(length)
    left = np.block([[real, -imag], [imag, real]])
    right = np.block([[real, imag], [-imag, real]])
    return np.asarray(left, np.float32), np.asarray(right, np.float32)


def halves(value):
    high = value.astype(jnp.bfloat16)
    return high, (value - high.astype(jnp.float32)).astype(jnp.bfloat16)


def mm(a, b):
    return jnp.dot(a, b, preferred_element_type=jnp.float32)


def left3(table_high, table_low, value):
    high, low = halves(value)
    return mm(table_high, high) + mm(table_high, low) + mm(table_low, high)


def right3(value, table_high, table_low):
    high, low = halves(value)
    return mm(high, table_high) + mm(low, table_high) + mm(high, table_low)


def remote(src, dst, send, recv, axis, target):
    return pltpu.make_async_remote_copy(
        src_ref=src, dst_ref=dst, send_sem=send, recv_sem=recv,
        device_id={axis: target}, device_id_type=MESH,
    )


def patch_kernel(n_pos, row_at, obj, offs, amp, probe, ah, al, bh, bl,
                 grad, from_above, from_below, offs_near, numden,
                 ext, q, psi, local_sem, send_sem, recv_sem):
    me = lax.axis_index("pos")
    up, down = lax.rem(me + n_pos - 1, n_pos), lax.rem(me + 1, n_pos)
    band = obj.shape[2]
    width = obj.shape[3]
    patch = probe.shape[1]
    half = patch // 2
    count = amp.shape[0]
    inner = pltpu.make_async_copy(obj.at[0], ext.at[:, pl.ds(half, band), :], local_sem.at[0])
    inner.start()
    barrier = pltpu.get_barrier_semaphore()
    for target in (up, down):
        pl.semaphore_signal(barrier, inc=1, device_id={"pos": target}, device_id_type=MESH)
    pl.semaphore_wait(barrier, 2)
    first = [
        remote(obj.at[0, :, pl.ds(band - half, half), :], ext.at[:, pl.ds(0, half), :],
               send_sem.at[0], recv_sem.at[0], "pos", down),
        remote(obj.at[0, :, pl.ds(0, half), :], ext.at[:, pl.ds(half + band, half), :],
               send_sem.at[1], recv_sem.at[1], "pos", up),
        remote(offs, offs_near.at[0], send_sem.at[2], recv_sem.at[2], "pos", down),
        remote(offs, offs_near.at[1], send_sem.at[3], recv_sem.at[3], "pos", up),
    ]
    for copy in first:
        copy.start()
    p_re, p_im = probe[0], probe[1]
    wide_at = lax.broadcasted_iota(jnp.int32, (width, count * patch), 0)
    pick_cols = (wide_at == offs[0:1, :]).astype(jnp.bfloat16)
    tall_at = lax.broadcasted_iota(jnp.int32, (patch, band + patch), 1)

    def choose(spans):
        parts = []
        for c in range(2):
            split = [halves(ext[c, span, :]) for span in spans]
            parts += [piece[0] for piece in split] + [piece[1] for piece in split]
        return mm(jnp.concatenate(parts, axis=0), pick_cols).astype(jnp.bfloat16)

    inner.wait()
    inside = choose((slice(half, half + band),))
    for copy in first:
        copy.wait()
    outer = choose((slice(0, half), slice(half + band, patch + band)))
    for j in range(count):
        pick_rows = (tall_at == row_at[j * patch:(j + 1) * patch, :]).astype(jnp.bfloat16)
        span = pl.ds(j * patch, patch)
        parts = []
        for k in range(4):
            parts += [outer[k * patch:k * patch + half, j * patch:(j + 1) * patch],
                      inside[k * band:(k + 1) * band, j * patch:(j + 1) * patch],
                      outer[k * patch + half:(k + 1) * patch, j * patch:(j + 1) * patch]]
        lines = [jnp.concatenate(parts[3 * k:3 * k + 3], axis=0) for k in range(4)]
        got = mm(pick_rows, jnp.concatenate(lines, axis=1))
        cut = [got[:, 2 * c * patch:(2 * c + 1) * patch] + got[:, (2 * c + 1) * patch:(2 * c + 2) * patch]
               for c in range(2)]
        q[0:patch, span] = cut[0]
        q[patch:, span] = cut[1]
        psi[0:patch, span] = p_re * cut[0] - p_im * cut[1]
        psi[patch:, span] = p_re * cut[1] + p_im * cut[0]
    mid = left3(ah[...], al[...], psi[...])
    rows = [
        jnp.concatenate(
            [mid[:patch, j * patch:(j + 1) * patch], mid[patch:, j * patch:(j + 1) * patch]], axis=1)
        for j in range(count)
    ]
    spec = right3(jnp.concatenate(rows, axis=0), bh[...], bl[...])
    fixed = []
    for j in range(count):
        s_re = spec[j * patch:(j + 1) * patch, :patch]
        s_im = spec[j * patch:(j + 1) * patch, patch:]
        factor = amp[j] / jnp.maximum(jnp.sqrt(s_re * s_re + s_im * s_im), 0.5)
        fixed.append(jnp.concatenate([factor * s_re, factor * s_im], axis=1))
    back = right3(jnp.concatenate(fixed, axis=0), ah[...], al[...])
    wide_re = jnp.concatenate([back[j * patch:(j + 1) * patch, :patch] for j in range(count)], axis=1)
    wide_im = jnp.concatenate([back[j * patch:(j + 1) * patch, patch:] for j in range(count)], axis=1)
    diff = left3(bh[...], bl[...], jnp.concatenate([wide_re, wide_im], axis=0)) - psi[...]
    n_re = jnp.zeros((patch, patch), jnp.float32)
    n_im = n_re
    den = n_re
    for j in range(count):
        lanes = slice(j * patch, (j + 1) * patch)
        d_re, d_im = diff[:patch, lanes], diff[patch:, lanes]
        g_re = p_re * d_re + p_im * d_im
        g_im = p_re * d_im - p_im * d_re
        for h in range(2):
            grad[h, 0, j] = g_re[h * half:(h + 1) * half]
            grad[h, 1, j] = g_im[h * half:(h + 1) * half]
        q_re, q_im = q[0:patch, lanes], q[patch:, lanes]
        n_re = n_re + (q_re * d_re + q_im * d_im)
        n_im = n_im + (q_re * d_im - q_im * d_re)
        den = den + (q_re * q_re + q_im * q_im)
    numden[0] = n_re
    numden[1] = n_im
    numden[2] = den
    second = [
        remote(grad.at[1], from_above, send_sem.at[4], recv_sem.at[4], "pos", down),
        remote(grad.at[0], from_below, send_sem.at[5], recv_sem.at[5], "pos", up),
    ]
    for copy in second:
        copy.start()
    for copy in second:
        copy.wait()


def merge_kernel(start_ref, own_ref, near_ref, obj, probe, grad, from_above, from_below,
                 out, acc):
    band = obj.shape[2]
    width = obj.shape[3]
    patch = probe.shape[1]
    half = patch // 2
    count = own_ref.shape[0]
    start = start_ref[0]
    acc[...] = jnp.zeros_like(acc)
    power = probe[0] * probe[0] + probe[1] * probe[1]
    last = acc.shape[1] - 8

    def place(planes, row, col):
        height = planes[0].shape[0]
        tile = jnp.minimum(col // 128, width // 128 - 2)
        base = pl.multiple_of(tile * 128, 128)
        shift = col - base
        top = pl.multiple_of(row // 8 * 8, 8)
        drop = row - top
        for c in range(3):
            tall = jnp.concatenate([planes[c], jnp.zeros((8, patch), jnp.float32)], axis=0)
            tall = pltpu.roll(tall, drop, 0)
            wide = jnp.concatenate([tall, jnp.zeros((height + 8, 128), jnp.float32)], axis=1)
            wide = pltpu.roll(wide, shift, 1)
            spot = (c, pl.ds(top, height + 8), pl.ds(base, 256))
            acc[spot] = acc[spot] + wide

    for j in range(count):
        planes = [jnp.concatenate([grad[0, c, j], grad[1, c, j]], axis=0) for c in range(2)]
        place(planes + [power], own_ref[j, 0] - start + patch, own_ref[j, 1])
    for side, ref in ((0, from_above), (1, from_below)):
        for j in range(count):
            row = near_ref[side, 1, j] - start + patch + (half if side == 0 else 0)
            col = near_ref[side, 0, j]

            @pl.when((row >= 0) & (row <= last - half))
            def _(side=side, ref=ref, j=j, row=row, col=col):
                part = power[half:] if side == 0 else power[:half]
                place([ref[0, j], ref[1, j], part], row, col)

    rows = pl.ds(patch, band)
    scale = acc[2, rows, :] + 1.0
    for c in range(2):
        out[0, c] = obj[0, c] + acc[c, rows, :] / scale


def final_kernel(n_ang, n_pos, new_obj, numden, probe, index, weight,
                 recon, newp,
                 sino, onehot, rh, rl, filt, rs, ag, piece,
                 local_sem, a2a_send, a2a_recv, rs_send, rs_recv, ag_send, ag_recv,
                 fin_send, fin_recv):
    me_a = lax.axis_index("angle")
    me_p = lax.axis_index("pos")
    ns = sino.shape[1]
    width = sino.shape[2]
    total = index.shape[1]
    pr = piece.shape[1]
    loads = [
        pltpu.make_async_copy(new_obj.at[0, 1, pl.ds(pl.multiple_of(me_a * ns, 8), ns), :],
                              sino.at[me_a], local_sem.at[0]),
    ]
    for copy in loads:
        copy.start()
    barrier = pltpu.get_barrier_semaphore()
    angle_peers = [lax.rem(me_a + d, n_ang) for d in range(1, n_ang)]
    pos_peers = [lax.rem(me_p + d, n_pos) for d in range(1, n_pos)]
    for peer in angle_peers:
        pl.semaphore_signal(barrier, inc=1, device_id={"angle": peer}, device_id_type=MESH)
    for peer in pos_peers:
        pl.semaphore_signal(barrier, inc=1, device_id={"pos": peer}, device_id_type=MESH)
    pl.semaphore_wait(barrier, n_ang + n_pos - 2)
    across = [
        remote(new_obj.at[0, 1, pl.ds(pl.multiple_of(peer * ns, 8), ns), :], sino.at[me_a],
               a2a_send.at[d], a2a_recv.at[d], "angle", peer)
        for d, peer in enumerate(angle_peers)
    ]
    for copy in across:
        copy.start()
    scatter = [
        remote(numden.at[:, pl.ds(pl.multiple_of(peer * pr, 8), pr), :], rs.at[d],
               rs_send.at[d], rs_recv.at[d], "pos", peer)
        for d, peer in enumerate(pos_peers)
    ]
    for copy in scatter:
        copy.start()

    chunk = 256
    bins = lax.broadcasted_iota(jnp.int32, (width, chunk), 0)

    def build(step, carry):
        a = step // (total // chunk)
        lanes = pl.ds(pl.multiple_of(lax.rem(step, total // chunk) * chunk, chunk), chunk)
        hit = bins == index[pl.ds(a, 1), lanes]
        onehot[a, :, lanes] = jnp.where(hit, 1.0, 0.0).astype(jnp.bfloat16)
        return carry

    lax.fori_loop(0, n_ang * (total // chunk), build, 0)

    tall = 64

    def ramp(step, carry):
        top = pl.multiple_of(step * tall, tall)
        shape = (tall, width)
        differ = lax.broadcasted_iota(jnp.int32, shape, 1) - (
            lax.broadcasted_iota(jnp.int32, shape, 0) + top)
        spread = differ.astype(jnp.float32)
        odd = -1.0 / (jnp.maximum(spread * spread, 1.0) * (math.pi * math.pi))
        value = jnp.where((differ & 1) == 1, odd, jnp.where(differ == 0, 0.25, 0.0))
        rh[pl.ds(top, tall), :], rl[pl.ds(top, tall), :] = halves(value)
        return carry

    lax.fori_loop(0, width // tall, ramp, 0)
    for copy in scatter:
        copy.wait()
    part = numden[:, pl.ds(pl.multiple_of(me_p * pr, 8), pr), :]
    for d in range(n_pos - 1):
        part = part + rs[d]
    ag[me_a] = part
    gather = [
        remote(ag.at[me_a], ag.at[me_a], ag_send.at[d], ag_recv.at[d], "angle", peer)
        for d, peer in enumerate(angle_peers)
    ]
    for copy in gather:
        copy.start()
    for copy in loads:
        copy.wait()
    for copy in across:
        copy.wait()

    rows = n_ang * ns
    high, low = halves(sino[...].reshape(rows, width))
    both = mm(jnp.concatenate([high, low], axis=0), rh[...])
    filtered = both[:rows] + both[rows:] + mm(high, rl[...])
    filt[...] = filtered.reshape(n_ang, ns, width)

    for copy in gather:
        copy.wait()
    whole = ag[0]
    for a in range(1, n_ang):
        whole = whole + ag[a]
    mine = pl.ds(pl.multiple_of(me_p * pr, 8), pr)
    for c in range(2):
        value = probe[c, mine, :] + whole[c] / (whole[2] + 1.0)
        piece[c] = value
        newp[c, mine, :] = value
    spread = [
        remote(piece, newp.at[:, mine, :], fin_send.at[d], fin_recv.at[d], "pos", peer)
        for d, peer in enumerate(pos_peers)
    ]
    for copy in spread:
        copy.start()

    recon[...] = jnp.zeros_like(recon)
    wide = 512

    def project(a, carry):
        lines = filt[a] * (math.pi / n_ang)
        high, low = halves(lines)
        next_high, next_low = halves(pltpu.roll(lines, width - 1, 1))
        stack = jnp.concatenate([high, low, next_high, next_low], axis=0)
        for n in range(total // wide):
            lanes = pl.ds(n * wide, wide)
            got = mm(stack, onehot[a, :, lanes])
            lower = got[:ns] + got[ns:2 * ns]
            upper = got[2 * ns:3 * ns] + got[3 * ns:]
            w = weight[pl.ds(a, 1), lanes]
            recon[:, lanes] += (1.0 - w) * lower + w * upper
        return carry

    lax.fori_loop(0, n_ang, project, 0)
    for copy in spread:
        copy.wait()


def on_device(n_ang, n_pos, amplitude, offsets, probe_field, object_field, interp_index, interp_weight):
    band = object_field.shape[2]
    width = object_field.shape[3]
    patch = probe_field.shape[1]
    half = patch // 2
    count = offsets.shape[1]
    f32, i32 = jnp.float32, jnp.int32
    start = lax.axis_index("pos").astype(i32) * band
    own = offsets[0]
    ramp = jnp.arange(patch, dtype=i32)[None, :]
    row_at = (own[:, :1] - (start - half) + ramp).reshape(count * patch, 1)
    lanes = (own[:, 1:] + ramp).reshape(1, count * patch)
    first_rows = (own[:, :1] + 0 * ramp).reshape(1, count * patch)
    padded = jnp.concatenate([lanes, first_rows, jnp.zeros((6, count * patch), i32)], axis=0)
    left, right = dft_blocks(patch)
    ah, al = split_const(left)
    bh, bl = split_const(right)
    vmem = pl.BlockSpec(memory_space=VMEM)
    smem = pl.BlockSpec(memory_space=pltpu.SMEM)
    hbm = pl.BlockSpec(memory_space=pl.ANY)
    sds = jax.ShapeDtypeStruct
    dma = pltpu.SemaphoreType.DMA
    half_shape = (2, count, half, patch)
    grad, from_above, from_below, near, numden = pl.pallas_call(
        functools.partial(patch_kernel, n_pos),
        out_shape=(
            sds((2,) + half_shape, f32), sds(half_shape, f32), sds(half_shape, f32),
            sds((2, 8, count * patch), i32), sds((3, patch, patch), f32),
        ),
        in_specs=[vmem, hbm] + [vmem] * 7,
        out_specs=(vmem,) * 5,
        scratch_shapes=[
            VMEM((2, band + patch, width), f32),
            VMEM((2 * patch, count * patch), f32),
            VMEM((2 * patch, count * patch), f32),
            dma((1,)), dma((6,)), dma((6,)),
        ],
        compiler_params=pltpu.CompilerParams(collective_id=0, has_side_effects=True),
        name="patches",
    )(row_at, object_field, padded, amplitude[0], probe_field, ah, al, bh, bl)
    new_object = pl.pallas_call(
        merge_kernel,
        out_shape=sds(object_field.shape, f32),
        in_specs=[smem] * 3 + [vmem] * 5,
        out_specs=vmem,
        scratch_shapes=[VMEM((3, band + 2 * patch + 8, width), f32)],
        name="merge",
    )(start[None], own, near[:, :2, ::patch], object_field, probe_field, grad, from_above, from_below)
    zwin = interp_index.shape[1]
    total = zwin * width
    ns = band // n_ang
    pr = patch // n_pos
    bf16 = jnp.bfloat16
    recon, new_probe = pl.pallas_call(
        functools.partial(final_kernel, n_ang, n_pos),
        out_shape=(sds((ns, total), f32), sds(probe_field.shape, f32)),
        in_specs=[hbm] + [vmem] * 4,
        out_specs=(vmem, vmem),
        scratch_shapes=[
            VMEM((n_ang, ns, width), f32),
            VMEM((n_ang, width, total), bf16),
            VMEM((width, width), bf16), VMEM((width, width), bf16),
            VMEM((n_ang, ns, width), f32),
            VMEM((n_pos - 1, 3, pr, patch), f32),
            VMEM((n_ang, 3, pr, patch), f32),
            VMEM((2, pr, patch), f32),
            dma((1,)),
            dma((n_ang - 1,)), dma((n_ang - 1,)),
            dma((n_pos - 1,)), dma((n_pos - 1,)),
            dma((n_ang - 1,)), dma((n_ang - 1,)),
            dma((n_pos - 1,)), dma((n_pos - 1,)),
        ],
        compiler_params=pltpu.CompilerParams(
            collective_id=1, has_side_effects=True, vmem_limit_bytes=BIG),
        name="final",
    )(new_object, numden, probe_field, interp_index.reshape(n_ang, total),
      interp_weight.reshape(n_ang, total))
    return new_object, new_probe, recon.reshape(1, ns, zwin, width)


def solution(mesh):
    placed = (
        P("angle", "pos", None, None),
        P("angle", "pos", None),
        P(),
        P("angle", None, "pos", None),
        P(),
        P(),
    )
    return jax.shard_map(
        functools.partial(on_device, mesh.shape["angle"], mesh.shape["pos"]),
        mesh=mesh,
        in_specs=placed,
        out_specs=(P("angle", None, "pos", None), P(), P("pos", "angle", None, None)),
        check_vma=False,
    )
```

time: 310 us -> 66.9 us (0.22)
  waiting for transfers between devices: 147 us -> 0 us
  Pallas kernels: 0 us -> 57.4 us
  matrix products: 45.6 us -> 0 us
  local copies, waits for them, and re-layouts: 45.6 us -> 7.71 us
  starting transfers between devices: 22.2 us -> 0 us
  other arithmetic: 17.6 us -> 0.76 us
  loops' own time: 15.4 us -> 0 us
  between operations: 14.4 us -> 0.68 us
    psum x1 -> x0, waiting for transfers between devices: 145 us -> none  [on_device(): lax.psum((jnp.sum(numers, axis=0), jnp.sum(denoms, axis=0)), ('angle', 'p...]
    pallas_call x0 -> x3, Pallas kernels: none -> 57.4 us  [the longest x1 29.1 us: on_device(): pl.pallas_call(functools.partial(patch_kernel, n_pos), out_shape=(sds((2,...]
    dot_general x25 -> x0, matrix products: 45.6 us -> none  [the longest x8 26.6 us: back_step(): results.append(jnp.dot(rows_angle, matrix, precision=lax.Precision.HIGHEST))]
    ppermute x4 -> x0, starting transfers between devices: 17.4 us -> none  [the longest x2 13.6 us: passed_along(): return lax.ppermute(array, axis, pairs)]
    another operation x3 -> x0, loops' own time: 15.4 us -> none  [the longest x1 15.2 us: one_angle(): lax.fori_loop(0, per_device, accumulate, jnp.zeros((channels, band + patc...]
    add x22 -> x2, other arithmetic: 11.3 us -> 0.08 us  [on_device(): lanes = (own[:, 1:] + ramp).reshape(1, count * patch)]
    dynamic_update_slice x4 -> x0, local copies, waits for them, and re-layouts: 11.2 us -> none  [accumulate(): return lax.dynamic_update_slice(total, current + stacked[count], start)]
    gather x12 -> x0, local copies, waits for them, and re-layouts: 10.2 us -> none
  transfers between devices with their start and end apart: 6 -> 0, of which waited for: 4 -> 0; matrix products, arithmetic and copies ran while one was open for 3% -> 0% of each run, Pallas kernels for 0% -> 0%
where the time goes in v1:
time: 66.9 us; the launch traced here: 66.6 us
  Pallas kernels  57.4 us (86%)
  local copies, waits for them, and re-layouts  7.71 us (12%)
  other arithmetic  0.76 us (1%)
  between operations  0.68 us (1%)
    pallas_call x1, Pallas kernels, on_device(): pl.pallas_call(functools.partial(patch_kernel, n_pos), out_shape=(sds((2,...  29.1 us
    pallas_call x1, Pallas kernels, on_device(): pl.pallas_call(functools.partial(final_kernel, n_ang, n_pos), out_shape=(...  24.4 us
    pallas_call x1, Pallas kernels, on_device(): pl.pallas_call(merge_kernel, out_shape=sds(object_field.shape, f32), in_s...  3.96 us
    unnamed x11, local copies, waits for them, and re-layouts  2.72 us
    reshape x1, local copies, waits for them, and re-layouts, on_device(): return (new_object, new_probe, recon.reshape(1, ns, zwin, width))  1.91 us
    slice x1, local copies, waits for them, and re-layouts, on_device(): near[:, :2, ::patch]  1.41 us

profile of v1, /device:TPU:0, one launch (start us, length us, event | category | flops | bytes accessed | tf_op | source)
XLA Modules:
  0.0 66.6 jit_solution(6387611974477055609)
XLA Ops:
  0.6 0.0 copy-start.3
  0.6 0.7 %copy-done.3 = s32[1,4,2]{1,2,0:T(2,128)S(1)} copy-done((s32[1,4,2]{1,2,0:T(2,128)S(1)}, s32[1,4,2]{1,2,0:T(2,128)}, u32[]{:S(2)}) %copy-start.3) | copy-done | bytes 56
  1.3 0.1 iota_add_fusion
  1.4 0.1 add.69
  1.5 0.1 pad.2.clone
  1.5 0.7 %add_add_fusion.offs = s32[8,512]{1,0:T(8,128)} fusion(s32[1,512]{1,0:T(1,128)S(1)} %bitcast.22, s32[1,512]{1,0:T(1,128)S(1)} %bitcast.23, s32[8]{0:T(128)S(1)} %pad.2.clone), kind=kLoop, calls=%fused_computation | loop fusion | flops 8192 | bytes 20512 | tf_op jit(solution)/shard_map/concatenate | solution.py:350
  2.2 0.9 %copy.14.row_at = s32[512,1]{1,0:T(8,128)} copy(s32[512,1]{0,1:T(1,128)S(1)} %bitcast.21) | data formatting | bytes 4096 | tf_op jit(solution)/shard_map/add | solution.py:347
  3.1 29.1 %patches.1 = (f32[2,2,4,64,128]{4,3,2,1,0:T(8,128)}, f32[2,4,64,128]{3,2,1,0:T(8,128)}, f32[2,4,64,128]{3,2,1,0:T(8,128)}, s32[2,8,512]{2,1,0:T(8,128)}, f32[3,128,128]{2,1,0:T(8,128)}) custom-call(s32[512,1]{1,0:T(8,128)} %copy.14.row_at, f32[1,2,128,1024]{3,2,1,0:T(8,128)} %obj.3, s32[8,512]{1,0:T(8,128)} %add_add_fusion.offs, f32[4,128,128]{2,1,0:T(8,128)} %bitcast.16, ...), custom_call_target="tpu_custom_call" | custom-call | tf_op jit(solution)/shard_map/patches/pallas_call | solution.py:360
  32.2 1.4 %slice.12.near_ref = s32[2,2,4]{2,1,0:T(2,128)} slice(s32[2,8,512]{2,1,0:T(8,128)} %get-tuple-element.10), slice={[0:2:1], [0:2:1], [0:512:128]} | slice | bytes 128 | tf_op jit(solution)/shard_map/slice | solution.py:384
  33.6 0.7 copy.15.own_ref
  34.3 0.0 copy-start.1
  34.3 4.0 %merge.1.new_obj = f32[1,2,128,1024]{3,2,1,0:T(8,128)} custom-call(s32[1]{0:T(128)} %bitcast.start_ref, s32[4,2]{1,0:T(4,128)} %copy.15.own_ref, s32[2,2,4]{2,1,0:T(2,128)} %slice.12.near_ref, f32[1,2,128,1024]{3,2,1,0:T(8,128)} %obj.3, f32[2,128,128]{2,1,0:T(8,128)} %probe.5, f32[2,2,4,64,128]{4,3,2,1,0:T(8,128)} %get-tuple-element.11.grad, ...), custom_call_target="tpu_custom_call" | custom-call | tf_op jit(solution)/shard_map/merge/pallas_call | solution.py:377
  38.3 0.0 copy-done.1
  38.3 0.0 copy-start.2
  38.3 0.6 copy.16
  38.9 0.1 copy-done.2
  39.0 0.6 copy.17
  39.6 24.4 %final.1 = (f32[32,2048]{1,0:T(8,128)}, f32[2,128,128]{2,1,0:T(8,128)}) custom-call(f32[1,2,128,1024]{3,2,1,0:T(8,128)} %merge.1.new_obj, f32[3,128,128]{2,1,0:T(8,128)} %get-tuple-element.14.numden, f32[2,128,128]{2,1,0:T(8,128)} %probe.5, s32[4,2048]{1,0:T(4,128)} %bitcast.17, f32[4,2048]{1,0:T(4,128)} %bitcast.18), custom_call_target="tpu_custom_call" | custom-call | tf_op jit(solution)/shard_map/final/pallas_call | solution.py:390
  64.0 0.0 copy-start
  64.0 1.9 %reshape.67 = f32[1,32,2,1024]{3,2,1,0:T(2,128)} reshape(f32[32,2048]{1,0:T(8,128)} %get-tuple-element.16) | data formatting | bytes 524288 | tf_op jit(solution)/shard_map/reshape | solution.py:414
  65.9 0.0 copy-done
  65.9 0.7 copy.19
  (2 shorter events, 0.0 us)
Async XLA Ops:
  0.6 0.7 %copy-start.3 = (s32[1,4,2]{1,2,0:T(2,128)S(1)}, s32[1,4,2]{1,2,0:T(2,128)}, u32[]{:S(2)}) copy-start(s32[1,4,2]{1,2,0:T(2,128)} %param.11) | copy-start | bytes 100
  34.3 4.0 %copy-start.1 = (s32[4,2,1024]{2,1,0:T(2,128)S(1)}, s32[4,2,1024]{2,1,0:T(2,128)}, u32[]{:S(2)}) copy-start(s32[4,2,1024]{2,1,0:T(2,128)} %param.14) | copy-start | bytes 98308
  38.3 0.8 %copy-start.2 = (f32[4,2,1024]{2,1,0:T(2,128)S(1)}, f32[4,2,1024]{2,1,0:T(2,128)}, u32[]{:S(2)}) copy-start(f32[4,2,1024]{2,1,0:T(2,128)} %param.15) | copy-start | bytes 98308
  64.0 1.9 %copy-start = (f32[2,128,128]{2,1,0:T(8,128)S(1)}, f32[2,128,128]{2,1,0:T(8,128)}, u32[]{:S(2)}) copy-start(f32[2,128,128]{2,1,0:T(8,128)} %get-tuple-element.26) | copy-start | bytes 393220

commit v2 on v1

v2 whole, which is shorter than its diff:
```python
import functools
import math

import jax
import jax.numpy as jnp
import numpy as np
from jax import lax
from jax.experimental import pallas as pl
from jax.experimental.pallas import tpu as pltpu
from jax.sharding import PartitionSpec as P

MESH = pl.DeviceIdType.MESH
VMEM = pltpu.VMEM
BIG = 60 * 1024 * 1024


def split_const(table):
    high = jnp.asarray(table, jnp.float32).astype(jnp.bfloat16)
    low = (jnp.asarray(table, jnp.float32) - high.astype(jnp.float32)).astype(jnp.bfloat16)
    return high, low


def dft_blocks(length):
    ramp = np.arange(length)
    theta = (ramp[:, None] * ramp[None, :] % length) * (2.0 * math.pi / length)
    real = np.cos(theta) / math.sqrt(length)
    imag = -np.sin(theta) / math.sqrt(length)
    left = np.block([[real, -imag], [imag, real]])
    right = np.block([[real, imag], [-imag, real]])
    return np.asarray(left, np.float32), np.asarray(right, np.float32)


def halves(value):
    high = value.astype(jnp.bfloat16)
    return high, (value - high.astype(jnp.float32)).astype(jnp.bfloat16)


def mm(a, b):
    return jnp.dot(a, b, preferred_element_type=jnp.float32)


def left3(table_high, table_low, value):
    high, low = halves(value)
    return mm(table_high, high) + mm(table_high, low) + mm(table_low, high)


def right3(value, table_high, table_low):
    high, low = halves(value)
    return mm(high, table_high) + mm(low, table_high) + mm(high, table_low)


def remote(src, dst, send, recv, axis, target):
    return pltpu.make_async_remote_copy(
        src_ref=src, dst_ref=dst, send_sem=send, recv_sem=recv,
        device_id={axis: target}, device_id_type=MESH,
    )


def patch_kernel(n_pos, where_at, obj, offs, index, amp, probe, ah, al, bh, bl,
                 grad, from_above, from_below, offs_near, partial, onehot,
                 ext, table, numden, rs,
                 local_sem, table_sem, send_sem, recv_sem, rs_send, rs_recv):
    me = lax.axis_index("pos")
    up, down = lax.rem(me + n_pos - 1, n_pos), lax.rem(me + 1, n_pos)
    band = obj.shape[2]
    width = obj.shape[3]
    patch = probe.shape[1]
    half = patch // 2
    count = amp.shape[0]
    inner = pltpu.make_async_copy(obj.at[0], ext.at[:, pl.ds(half, band), :], local_sem.at[0])
    inner.start()
    barrier = pltpu.get_barrier_semaphore()
    pos_peers = [lax.rem(me + d, n_pos) for d in range(1, n_pos)]
    for target in pos_peers:
        pl.semaphore_signal(barrier, inc=1, device_id={"pos": target}, device_id_type=MESH)
    pl.semaphore_wait(barrier, n_pos - 1)
    first = [
        remote(obj.at[0, :, pl.ds(band - half, half), :], ext.at[:, pl.ds(0, half), :],
               send_sem.at[0], recv_sem.at[0], "pos", down),
        remote(obj.at[0, :, pl.ds(0, half), :], ext.at[:, pl.ds(half + band, half), :],
               send_sem.at[1], recv_sem.at[1], "pos", up),
        remote(offs, offs_near.at[0], send_sem.at[2], recv_sem.at[2], "pos", down),
        remote(offs, offs_near.at[1], send_sem.at[3], recv_sem.at[3], "pos", up),
    ]
    for copy in first:
        copy.start()
    p_re, p_im = probe[0], probe[1]
    wide_at = lax.broadcasted_iota(jnp.int32, (width, count * patch), 0)
    pick_cols = (wide_at == where_at[0:1, :]).astype(jnp.bfloat16)
    tall_at = lax.broadcasted_iota(jnp.int32, (patch, band + patch), 1)

    def choose(spans):
        parts = []
        for c in range(2):
            split = [halves(ext[c, span, :]) for span in spans]
            parts += [piece[0] for piece in split] + [piece[1] for piece in split]
        return mm(jnp.concatenate(parts, axis=0), pick_cols).astype(jnp.bfloat16)

    inner.wait()
    inside = choose((slice(half, half + band),))
    chunk = table.shape[2]
    per_row = width // chunk
    zwin = index.shape[1]
    steps = onehot.shape[0]
    bins = lax.broadcasted_iota(jnp.int32, (width, chunk), 0)

    def shipped(step, slot):
        return pltpu.make_async_copy(table.at[slot], onehot.at[step], table_sem.at[slot])

    def build(step, slot):
        a = step // (zwin * per_row)
        z = lax.rem(step // per_row, zwin)
        lanes = pl.ds(pl.multiple_of(lax.rem(step, per_row) * chunk, chunk), chunk)
        hit = bins == index[a, pl.ds(z, 1), lanes]
        table[slot] = jnp.where(hit, 1.0, 0.0).astype(jnp.bfloat16)
        shipped(step, slot).start()

    def build_pair(pair, carry):
        for slot in range(2):
            shipped(2 * pair + slot - 2, slot).wait()
            build(2 * pair + slot, slot)
        return carry

    for slot in range(2):
        build(jnp.int32(slot), slot)
    lax.fori_loop(1, steps // 2, build_pair, 0)
    for copy in first:
        copy.wait()
    outer = choose((slice(0, half), slice(half + band, patch + band)))
    n_re = jnp.zeros((patch, patch), jnp.float32)
    n_im = n_re
    den = n_re
    second = []
    size = 2 if count % 2 == 0 else count
    for g in range(count // size):
        group = range(g * size, (g + 1) * size)
        q_re, q_im, w_re, w_im = [], [], [], []
        for j in group:
            row_at = jnp.broadcast_to(where_at[1:2, j * patch:(j + 1) * patch], (patch, patch))
            row_at = jnp.transpose(row_at)[:, :1]
            pick_rows = (tall_at == row_at).astype(jnp.bfloat16)
            parts = []
            for k in range(4):
                parts += [outer[k * patch:k * patch + half, j * patch:(j + 1) * patch],
                          inside[k * band:(k + 1) * band, j * patch:(j + 1) * patch],
                          outer[k * patch + half:(k + 1) * patch, j * patch:(j + 1) * patch]]
            lines = [jnp.concatenate(parts[3 * k:3 * k + 3], axis=0) for k in range(4)]
            got = mm(pick_rows, jnp.concatenate(lines, axis=1))
            re = got[:, :patch] + got[:, patch:2 * patch]
            im = got[:, 2 * patch:3 * patch] + got[:, 3 * patch:]
            q_re.append(re)
            q_im.append(im)
            w_re.append(p_re * re - p_im * im)
            w_im.append(p_re * im + p_im * re)
        psi = jnp.concatenate([jnp.concatenate(w_re, axis=1), jnp.concatenate(w_im, axis=1)], axis=0)
        mid = left3(ah[...], al[...], psi)
        cells = [slice(n * patch, (n + 1) * patch) for n in range(size)]
        rows = [jnp.concatenate([mid[:patch, cell], mid[patch:, cell]], axis=1) for cell in cells]
        spec = right3(jnp.concatenate(rows, axis=0), bh[...], bl[...])
        fixed = []
        for j, cell in zip(group, cells):
            s_re = spec[cell, :patch]
            s_im = spec[cell, patch:]
            factor = amp[j] / jnp.maximum(jnp.sqrt(s_re * s_re + s_im * s_im), 0.5)
            fixed.append(jnp.concatenate([factor * s_re, factor * s_im], axis=1))
        back = right3(jnp.concatenate(fixed, axis=0), ah[...], al[...])
        wide_re = jnp.concatenate([back[cell, :patch] for cell in cells], axis=1)
        wide_im = jnp.concatenate([back[cell, patch:] for cell in cells], axis=1)
        diff = left3(bh[...], bl[...], jnp.concatenate([wide_re, wide_im], axis=0))
        diff = diff - psi
        for n, j in enumerate(group):
            d_re, d_im = diff[:patch, cells[n]], diff[patch:, cells[n]]
            g_re = p_re * d_re + p_im * d_im
            g_im = p_re * d_im - p_im * d_re
            for h in range(2):
                grad[h, j, 0] = g_re[h * half:(h + 1) * half]
                grad[h, j, 1] = g_im[h * half:(h + 1) * half]
            n_re = n_re + (q_re[n] * d_re + q_im[n] * d_im)
            n_im = n_im + (q_re[n] * d_im - q_im[n] * d_re)
            den = den + (q_re[n] * q_re[n] + q_im[n] * q_im[n])
        if g == count // size - 1:
            numden[0] = n_re
            numden[1] = n_im
            numden[2] = den
        span = pl.ds(g * size, size)
        sems = [4 + 2 * g, 5 + 2 * g]
        pair = [
            remote(grad.at[1, span], from_above.at[span], send_sem.at[sems[0]],
                   recv_sem.at[sems[0]], "pos", down),
            remote(grad.at[0, span], from_below.at[span], send_sem.at[sems[1]],
                   recv_sem.at[sems[1]], "pos", up),
        ]
        for copy in pair:
            copy.start()
        second += pair
    pr = patch // n_pos
    scatter = [
        remote(numden.at[:, pl.ds(pl.multiple_of(peer * pr, 8), pr), :], rs.at[d],
               rs_send.at[d], rs_recv.at[d], "pos", peer)
        for d, peer in enumerate(pos_peers)
    ]
    for copy in scatter:
        copy.start()
    for slot in range(2):
        shipped(steps - 2 + slot, slot).wait()
    for copy in scatter:
        copy.wait()
    part = numden[:, pl.ds(pl.multiple_of(me * pr, 8), pr), :]
    for d in range(n_pos - 1):
        part = part + rs[d]
    partial[...] = part
    for copy in second:
        copy.wait()


def merge_kernel(count, start_ref, own_ref, near_ref, obj, probe, grad, from_above, from_below,
                 out, acc):
    band = obj.shape[2]
    width = obj.shape[3]
    patch = probe.shape[1]
    half = patch // 2
    start = start_ref[0]
    acc[...] = jnp.zeros_like(acc)
    power = probe[0] * probe[0] + probe[1] * probe[1]
    last = acc.shape[1] - 8

    def place(planes, row, col):
        height = planes[0].shape[0]
        tile = jnp.minimum(col // 128, width // 128 - 2)
        base = pl.multiple_of(tile * 128, 128)
        shift = col - base
        top = pl.multiple_of(row // 8 * 8, 8)
        drop = row - top
        for c in range(3):
            tall = jnp.concatenate([planes[c], jnp.zeros((8, patch), jnp.float32)], axis=0)
            tall = pltpu.roll(tall, drop, 0)
            wide = jnp.concatenate([tall, jnp.zeros((height + 8, 128), jnp.float32)], axis=1)
            wide = pltpu.roll(wide, shift, 1)
            spot = (c, pl.ds(top, height + 8), pl.ds(base, 256))
            acc[spot] = acc[spot] + wide

    for j in range(count):
        planes = [jnp.concatenate([grad[0, j, c], grad[1, j, c]], axis=0) for c in range(2)]
        place(planes + [power], own_ref[0, 2 * j] - start + patch, own_ref[0, 2 * j + 1])
    for side, ref in ((0, from_above), (1, from_below)):
        for j in range(count):
            row = near_ref[side, 0, 2 * j] - start + patch + (half if side == 0 else 0)
            col = near_ref[side, 0, 2 * j + 1]

            @pl.when((row >= 0) & (row <= last - half))
            def _(side=side, ref=ref, j=j, row=row, col=col):
                part = power[half:] if side == 0 else power[:half]
                place([ref[j, 0], ref[j, 1], part], row, col)

    rows = pl.ds(patch, band)
    scale = acc[2, rows, :] + 1.0
    for c in range(2):
        out[0, c] = obj[0, c] + acc[c, rows, :] / scale


def final_kernel(n_ang, n_pos, new_obj, partial, weight, onehot,
                 recon, newp,
                 sino, tables, rh, rl, ag, piece,
                 local_sem, table_sem, a2a_send, a2a_recv, ag_send, ag_recv,
                 fin_send, fin_recv):
    me_a = lax.axis_index("angle")
    me_p = lax.axis_index("pos")
    ns = sino.shape[1]
    width = sino.shape[2]
    pr = piece.shape[1]
    chunk = tables.shape[2]
    per_row = width // chunk
    zwin = weight.shape[1]
    per_angle = zwin * per_row
    order = sorted(range(1, n_ang), key=lambda d: (min(d, n_ang - d), d))
    barrier = pltpu.get_barrier_semaphore()
    angle_peers = [lax.rem(me_a + d, n_ang) for d in order]
    pos_peers = [lax.rem(me_p + d, n_pos) for d in range(1, n_pos)]
    for peer in angle_peers:
        pl.semaphore_signal(barrier, inc=1, device_id={"angle": peer}, device_id_type=MESH)
    for peer in pos_peers:
        pl.semaphore_signal(barrier, inc=1, device_id={"pos": peer}, device_id_type=MESH)
    own = pltpu.make_async_copy(new_obj.at[0, 1, pl.ds(pl.multiple_of(me_a * ns, 8), ns), :],
                                sino.at[me_a], local_sem.at[0])
    own.start()
    sources = [me_a] + [lax.rem(me_a + n_ang - d, n_ang) for d in order]
    loads = []
    for k, a in enumerate(sources):
        span = pl.ds(a * per_angle, per_angle)
        loads.append(pltpu.make_async_copy(onehot.at[span], tables.at[span], table_sem.at[k]))
    loads[0].start()
    pl.semaphore_wait(barrier, n_ang + n_pos - 2)
    gather = [
        remote(partial, ag.at[me_a], ag_send.at[k], ag_recv.at[k], "angle", peer)
        for k, peer in enumerate(angle_peers)
    ]
    for copy in gather:
        copy.start()
    across = [
        remote(new_obj.at[0, 1, pl.ds(pl.multiple_of(peer * ns, 8), ns), :], sino.at[me_a],
               a2a_send.at[k], a2a_recv.at[k], "angle", peer)
        for k, peer in enumerate(angle_peers)
    ]
    for copy in across:
        copy.start()
    for copy in loads[1:]:
        copy.start()
    tall = 64

    def ramp(step, carry):
        top = pl.multiple_of(step * tall, tall)
        shape = (tall, width)
        differ = lax.broadcasted_iota(jnp.int32, shape, 1) - (
            lax.broadcasted_iota(jnp.int32, shape, 0) + top)
        spread = differ.astype(jnp.float32)
        odd = -1.0 / (jnp.maximum(spread * spread, 1.0) * (math.pi * math.pi))
        value = jnp.where((differ & 1) == 1, odd, jnp.where(differ == 0, 0.25, 0.0))
        rh[pl.ds(top, tall), :], rl[pl.ds(top, tall), :] = halves(value)
        return carry

    lax.fori_loop(0, width // tall, ramp, 0)

    def project(k):
        a = sources[k]
        high, low = halves(sino[a])
        both = mm(jnp.concatenate([high, low], axis=0), rh[...])
        lines = (both[:ns] + both[ns:] + mm(high, rl[...])) * (math.pi / n_ang)
        high, low = halves(lines)
        next_high, next_low = halves(pltpu.roll(lines, width - 1, 1))
        stack = jnp.concatenate([high, low, next_high, next_low], axis=0)
        loads[k].wait()
        for n in range(per_angle):
            z, part = n // per_row, n % per_row
            got = mm(stack, tables[a * per_angle + n])
            lower = got[:ns] + got[ns:2 * ns]
            upper = got[2 * ns:3 * ns] + got[3 * ns:]
            w = weight[pl.ds(a, 1), z, pl.ds(part * chunk, chunk)]
            value = (1.0 - w) * lower + w * upper
            lanes = pl.ds(n * chunk, chunk)
            recon[:, lanes] = value if k == 0 else recon[:, lanes] + value

    ag[me_a] = partial[...]
    for copy in gather:
        copy.wait()
    mine = pl.ds(pl.multiple_of(me_p * pr, 8), pr)
    whole = ag[0]
    for a in range(1, n_ang):
        whole = whole + ag[a]
    for c in range(2):
        value = whole[c] / (whole[2] + 1.0)
        piece[c] = value
        newp[c, mine, :] = value
    spread = [
        remote(piece, newp.at[:, mine, :], fin_send.at[d], fin_recv.at[d], "pos", peer)
        for d, peer in enumerate(pos_peers)
    ]
    for copy in spread:
        copy.start()
    own.wait()
    project(0)
    for k in range(1, n_ang):
        across[k - 1].wait()
        project(k)
    for copy in spread:
        copy.wait()


def on_device(n_ang, n_pos, amplitude, offsets, probe_field, object_field, interp_index, interp_weight):
    band = object_field.shape[2]
    width = object_field.shape[3]
    patch = probe_field.shape[1]
    half = patch // 2
    count = offsets.shape[1]
    f32, i32 = jnp.float32, jnp.int32
    start = lax.axis_index("pos").astype(i32) * band
    own = offsets[0]
    corner = own.T - jnp.where(jnp.arange(2)[:, None] == 0, start - half, 0)
    where_at = corner[::-1, :, None] + jnp.arange(patch, dtype=i32)[None, None, :]
    where_at = where_at.reshape(2, count * patch)
    padded = jnp.pad(own.reshape(1, 2 * count), ((0, 7), (0, 128 - 2 * count)))
    n_z = interp_index.shape[1]
    chunk = min(512, width)
    tables = n_ang * n_z * (width // chunk)
    bf16 = jnp.bfloat16
    left, right = dft_blocks(patch)
    ah, al = split_const(left)
    bh, bl = split_const(right)
    vmem = pl.BlockSpec(memory_space=VMEM)
    smem = pl.BlockSpec(memory_space=pltpu.SMEM)
    hbm = pl.BlockSpec(memory_space=pl.ANY)
    sds = jax.ShapeDtypeStruct
    dma = pltpu.SemaphoreType.DMA
    half_shape = (count, 2, half, patch)
    grad, from_above, from_below, near, partial, onehot = pl.pallas_call(
        functools.partial(patch_kernel, n_pos),
        out_shape=(
            sds((2,) + half_shape, f32), sds(half_shape, f32), sds(half_shape, f32),
            sds((2, 8, 128), i32), sds((3, patch // n_pos, patch), f32),
            sds((tables, width, chunk), bf16),
        ),
        in_specs=[vmem, hbm] + [vmem] * 8,
        out_specs=(vmem,) * 5 + (hbm,),
        scratch_shapes=[
            VMEM((2, band + patch, width), f32),
            VMEM((2, width, chunk), bf16),
            VMEM((3, patch, patch), f32),
            VMEM((n_pos - 1, 3, patch // n_pos, patch), f32),
            dma((1,)), dma((2,)), dma((4 + 2 * count,)), dma((4 + 2 * count,)), dma((n_pos - 1,)), dma((n_pos - 1,)),
        ],
        compiler_params=pltpu.CompilerParams(collective_id=0, has_side_effects=True),
        name="patches",
    )(where_at, object_field, padded, interp_index, amplitude[0], probe_field, ah, al, bh, bl)
    new_object = pl.pallas_call(
        functools.partial(merge_kernel, count),
        out_shape=sds(object_field.shape, f32),
        in_specs=[smem] * 3 + [vmem] * 5,
        out_specs=vmem,
        scratch_shapes=[VMEM((3, band + 2 * patch + 8, width), f32)],
        name="merge",
    )(start[None], padded, near, object_field, probe_field, grad, from_above, from_below)
    total = n_z * width
    ns = band // n_ang
    pr = patch // n_pos
    recon, change = pl.pallas_call(
        functools.partial(final_kernel, n_ang, n_pos),
        out_shape=(sds((ns, total), f32), sds(probe_field.shape, f32)),
        in_specs=[hbm] + [vmem] * 2 + [hbm],
        out_specs=(vmem, vmem),
        scratch_shapes=[
            VMEM((n_ang, ns, width), f32),
            VMEM((tables, width, chunk), bf16),
            VMEM((width, width), bf16), VMEM((width, width), bf16),
            VMEM((n_ang, 3, pr, patch), f32),
            VMEM((2, pr, patch), f32),
            dma((1,)), dma((n_ang,)),
            dma((n_ang - 1,)), dma((n_ang - 1,)),
            dma((n_ang - 1,)), dma((n_ang - 1,)),
            dma((n_pos - 1,)), dma((n_pos - 1,)),
        ],
        compiler_params=pltpu.CompilerParams(
            collective_id=1, has_side_effects=True, vmem_limit_bytes=BIG),
        name="final",
    )(new_object, partial, interp_weight, onehot)
    return new_object, probe_field + change, recon.reshape(1, ns, n_z, width)


def solution(mesh):
    placed = (
        P("angle", "pos", None, None),
        P("angle", "pos", None),
        P(),
        P("angle", None, "pos", None),
        P(),
        P(),
    )
    return jax.shard_map(
        functools.partial(on_device, mesh.shape["angle"], mesh.shape["pos"]),
        mesh=mesh,
        in_specs=placed,
        out_specs=(P("angle", None, "pos", None), P(), P("pos", "angle", None, None)),
        check_vma=False,
    )
```

time: 66.9 us -> 65 us (0.972)
  local copies, waits for them, and re-layouts: 7.71 us -> 3.42 us
  other arithmetic: 0.76 us -> 2.97 us
    pallas_call x1, Pallas kernels: 29.1 us -> 31.4 us  [on_device(): pl.pallas_call(functools.partial(patch_kernel, n_pos), out_shape=(sds((2,...]
    add x2, other arithmetic: 0.08 us -> 2.18 us  [the longest x1 1.57 us: on_device(): return (new_object, probe_field + change, recon.reshape(1, ns, n_z, width))]
    pallas_call x1, Pallas kernels: 24.4 us -> 22.3 us  [on_device(): pl.pallas_call(functools.partial(final_kernel, n_ang, n_pos), out_shape=(...]
    unnamed x11 -> x4, local copies, waits for them, and re-layouts: 2.72 us -> 0.84 us
    slice x1 -> x0, local copies, waits for them, and re-layouts: 1.41 us -> none  [on_device(): near[:, :2, ::patch]]
    add x2 -> x1, local copies, waits for them, and re-layouts: 0.93 us -> 0.01 us  [on_device(): corner[::-1, :, None] + jnp.arange(patch, dtype=i32)[None, None, :]]
    sub x0 -> x1, other arithmetic: none -> 0.78 us  [on_device(): corner = own.T - jnp.where(jnp.arange(2)[:, None] == 0, start - half, 0)]
    concatenate x1 -> x0, other arithmetic: 0.68 us -> none  [on_device(): jnp.concatenate([lanes, first_rows, jnp.zeros((6, count * patch), i32)],...]
where the time goes in v2:
time: 65 us; the launch traced here: 64.7 us
  Pallas kernels  57.6 us (89%)
  local copies, waits for them, and re-layouts  3.42 us (5%)
  other arithmetic  2.97 us (5%)
  between operations  0.68 us (1%)
    pallas_call x1, Pallas kernels, on_device(): pl.pallas_call(functools.partial(patch_kernel, n_pos), out_shape=(sds((2,...  31.4 us
    pallas_call x1, Pallas kernels, on_device(): pl.pallas_call(functools.partial(final_kernel, n_ang, n_pos), out_shape=(...  22.3 us
    pallas_call x1, Pallas kernels, on_device(): pl.pallas_call(functools.partial(merge_kernel, count), out_shape=sds(obje...  3.95 us
    reshape x1, local copies, waits for them, and re-layouts, on_device(): return (new_object, probe_field + change, recon.reshape(1, ns, n_z, width))  1.87 us
    add x1, other arithmetic, on_device(): return (new_object, probe_field + change, recon.reshape(1, ns, n_z, width))  1.57 us

profile of v2, /device:TPU:0, one launch (start us, length us, event | category | flops | bytes accessed | tf_op | source)
XLA Modules:
  0.0 64.7 jit_solution(13878417831856145351)
XLA Ops:
  0.6 0.0 copy-start
  0.7 0.8 %fusion = s32[2,4]{1,0:T(2,128)S(1)} fusion(s32[1,4,2]{1,2,0:T(2,128)} %param.11, s32[2]{0:T(128)S(1)} %compare_select_fusion), kind=kLoop, calls=%fused_computation.5 | loop fusion | flops 8 | bytes 72 | tf_op jit(solution)/shard_map/sub | solution.py:377
  1.5 0.8 %copy.14 = s32[1,4,2]{2,1,0:T(4,128)S(1)} copy(s32[1,4,2]{1,2,0:T(2,128)} %param.11) | data formatting | bytes 64 | tf_op args[1]
  2.2 0.1 reshape_squeeze.3
  2.3 0.1 broadcast_bitcast_fusion
  2.4 0.6 bitcast_add_fusion.where_at
  3.0 0.6 pad.4.offs.own_ref
  3.6 31.4 %patches.1 = (f32[2,4,2,64,128]{4,3,2,1,0:T(8,128)}, f32[4,2,64,128]{3,2,1,0:T(8,128)}, f32[4,2,64,128]{3,2,1,0:T(8,128)}, s32[2,8,128]{2,1,0:T(8,128)}, f32[3,1...) custom-call(s32[2,512]{1,0:T(2,128)} %bitcast_add_fusion.where_at, f32[1,2,128,1024]{3,2,1,0:T(8,128)} %obj.3, ...), custom_call_target="tpu_custom_call" | custom-call | tf_op jit(solution)/shard_map/patches/pallas_call | solution.py:394
  35.0 4.0 %merge.1.new_obj = f32[1,2,128,1024]{3,2,1,0:T(8,128)} custom-call(s32[1]{0:T(128)} %bitcast.start_ref, s32[8,128]{1,0:T(8,128)} %pad.4.offs.own_ref, s32[2,8,128]{2,1,0:T(8,128)} %get-tuple-element.11.near_ref, f32[1,2,128,1024]{3,2,1,0:T(8,128)} %obj.3, f32[2,128,128]{2,1,0:T(8,128)} %probe.3, f32[2,4,2,64,128]{4,3,2,1,0:T(8,128)} %get-tuple-element.12.grad, ...), custom_call_target="tpu_custom_call" | custom-call | tf_op jit(solution)/shard_map/merge/pallas_call | solution.py:413
  38.9 22.3 %final.1 = (f32[32,2048]{1,0:T(8,128)}, f32[2,128,128]{2,1,0:T(8,128)}) custom-call(f32[1,2,128,1024]{3,2,1,0:T(8,128)} %merge.1.new_obj, f32[3,16,128]{2,1,0:T(8,128)} %get-tuple-element.15.partial, f32[4,2,1024]{2,1,0:T(2,128)} %weight.1, bf16[16,1024,512]{2,1,0:T(8,128)(2,1)} %get-tuple-element.16.onehot), custom_call_target="tpu_custom_call" | custom-call | tf_op jit(solution)/shard_map/final/pallas_call | solution.py:424
  61.2 0.0 copy-done
  61.2 1.6 %add.32 = f32[2,128,128]{2,1,0:T(8,128)} add(f32[2,128,128]{2,1,0:T(8,128)S(1)} %copy-done, f32[2,128,128]{2,1,0:T(8,128)} %get-tuple-element.17) | non-fusion elementwise | flops 32768 | bytes 393216 | tf_op jit(solution)/shard_map/add | solution.py:444
  62.8 1.9 %reshape.20 = f32[1,32,2,1024]{3,2,1,0:T(2,128)} reshape(f32[32,2048]{1,0:T(8,128)} %get-tuple-element.18) | data formatting | bytes 524288 | tf_op jit(solution)/shard_map/reshape | solution.py:444
  (3 shorter events, 0.0 us)
Async XLA Ops:
  0.6 60.6 %copy-start = (f32[2,128,128]{2,1,0:T(8,128)S(1)}, f32[2,128,128]{2,1,0:T(8,128)}, u32[]{:S(2)}) copy-start(f32[2,128,128]{2,1,0:T(8,128)} %probe.3) | copy-start | bytes 393220
